TPU v7x, 32 devices: a whole 2x2x4 slice. The times are simulated.
32 devices in a mesh: freq: 32 (over z, y, x, core).
Axes of the slice: x: 2, y: 2, z: 4, core: 2. Of those that a mesh axis runs over, the one named last changes fastest.
Arguments:
- pulses: float32 [1, 2, 30, 65536], P(None, None, None, 'freq'), may hold values from -4 to 4
- coupling: float32 [2, 30, 30, 65536], P(None, None, None, 'freq'), may hold values from -0.4 to 0.4
- dispersion_terms: float32 [3, 30], replicated, may hold values from -3 to 3
- kerr_gain: float32 [30], replicated, may hold values from 0.01 to 0.08
Outputs:
- evolved: float32 [1, 2, 30, 65536], P(None, None, None, 'freq')
All inputs are finite; a program needn't handle non-finite values.
Results may differ from a plain program's by a relative error of at most 0.00027.
Values sent between devices are 32-bit elements; how exact they have to be, the bound alone decides.
A program may use at most 128 MiB of HBM per device.

v0:
```python
import jax
import jax.numpy as jnp
from jax import lax
from jax.sharding import PartitionSpec as P

STEPS = 2


HIGHEST = lax.Precision.HIGHEST


def angle_table(first, second, modulus, orient):
    turns = first[:, None] * second[None, :] % modulus
    radians = turns.astype(jnp.float32) * (2.0 * jnp.pi / modulus)
    return (jnp.cos(radians), orient * jnp.sin(radians))


def rotate(real_part, imag_part, cosine, sine):
    return (real_part * cosine - imag_part * sine, real_part * sine + imag_part * cosine)


def transform(stacked, cosine, sine):
    real_part = stacked[:, 0]
    imag_part = stacked[:, 1]
    out_real = jnp.matmul(real_part, cosine, precision=HIGHEST) - jnp.matmul(
        imag_part, sine, precision=HIGHEST
    )
    out_imag = jnp.matmul(real_part, sine, precision=HIGHEST) + jnp.matmul(
        imag_part, cosine, precision=HIGHEST
    )
    return jnp.stack((out_real, out_imag), axis=1)


def nonlinear_phase(stacked, kerr_gain):
    magnitude = stacked[:, 0] ** 2 + stacked[:, 1] ** 2
    total_power = jnp.sum(magnitude, axis=1, keepdims=True)
    gains = kerr_gain.reshape((1, -1) + (1,) * (magnitude.ndim - 2))
    angles = gains * (2.0 * total_power - magnitude)
    real_part, imag_part = rotate(stacked[:, 0], stacked[:, 1], jnp.cos(angles), jnp.sin(angles))
    return jnp.stack((real_part, imag_part), axis=1)


def per_device(pulses, coupling, dispersion_terms, kerr_gain):
    shards = lax.axis_size("freq")
    device = lax.axis_index("freq")
    mode_count = pulses.shape[2]
    local_count = pulses.shape[3]
    groups = local_count // shards
    total_count = local_count * shards
    column_index = jnp.arange(shards, dtype=jnp.int32)
    row_index = jnp.arange(local_count, dtype=jnp.int32)
    short_cos, short_sin = angle_table(column_index, column_index, shards, -1.0)
    inverse_short_cos, inverse_short_sin = angle_table(column_index, column_index, shards, 1.0)
    long_cos, long_sin = angle_table(row_index, row_index, local_count, -1.0)
    inverse_long_cos, inverse_long_sin = angle_table(row_index, row_index, local_count, 1.0)
    sample_rows = jnp.arange(groups, dtype=jnp.int32) * shards + device
    twist_cos, twist_sin = angle_table(sample_rows, column_index, total_count, -1.0)
    untwist_cos, untwist_sin = angle_table(row_index, jnp.reshape(device, (1,)), total_count, 1.0)
    untwist_cos = untwist_cos.reshape(-1)
    untwist_sin = untwist_sin.reshape(-1)
    bins = device + shards * row_index
    signed_bin = jnp.where(bins < total_count // 2, bins, bins - total_count).astype(jnp.float32)
    angular = signed_bin / (total_count // 2)
    dispersion = (
        dispersion_terms[0][:, None] * angular
        + dispersion_terms[1][:, None] * angular**2 / 2
        + dispersion_terms[2][:, None] * angular**3 / 6
    )
    spread_cos = jnp.cos(dispersion)
    spread_sin = jnp.sin(dispersion)
    identity = jnp.eye(mode_count, dtype=jnp.float32)[:, :, None]
    mixing_real = coupling[0] + identity
    mixing_imag = coupling[1]
    blocks = pulses.reshape(pulses.shape[0], 2, mode_count, groups, shards)
    columns = lax.all_to_all(blocks, "freq", split_axis=4, concat_axis=4, tiled=True)
    for repeat in range(STEPS):
        spectral = transform(columns, short_cos, short_sin)
        forward_real_part, forward_imag_part = rotate(
            spectral[:, 0], spectral[:, 1], twist_cos, twist_sin
        )
        evolve_rows = lax.all_to_all(
            jnp.stack((forward_real_part, forward_imag_part), axis=1),
            "freq",
            split_axis=4,
            concat_axis=4,
            tiled=True,
        )
        flat = evolve_rows.reshape(evolve_rows.shape[0], 2, mode_count, local_count)
        spectrum = transform(flat, long_cos, long_sin)
        spec_real = spectrum[:, 0]
        spec_imag = spectrum[:, 1]
        mixed_real = jnp.einsum(
            "nmk,bmk->bnk", mixing_real, spec_real, precision=HIGHEST
        ) - jnp.einsum("nmk,bmk->bnk", mixing_imag, spec_imag, precision=HIGHEST)
        mixed_imag = jnp.einsum(
            "nmk,bmk->bnk", mixing_real, spec_imag, precision=HIGHEST
        ) + jnp.einsum("nmk,bmk->bnk", mixing_imag, spec_real, precision=HIGHEST)
        real_part, imag_part = rotate(mixed_real, mixed_imag, spread_cos, spread_sin)
        inverted = transform(
            jnp.stack((real_part, imag_part), axis=1), inverse_long_cos, inverse_long_sin
        )
        real_part, imag_part = rotate(inverted[:, 0], inverted[:, 1], untwist_cos, untwist_sin)
        moved = jnp.stack((real_part, imag_part), axis=1).reshape(evolve_rows.shape)
        columns = nonlinear_phase(
            transform(
                lax.all_to_all(moved, "freq", split_axis=4, concat_axis=4, tiled=True),
                inverse_short_cos,
                inverse_short_sin,
            )
            * (1.0 / total_count),
            kerr_gain,
        )
    returned = lax.all_to_all(columns, "freq", split_axis=4, concat_axis=4, tiled=True)
    return returned.reshape(columns.shape[0], 2, mode_count, local_count)


def solution(mesh):
    in_specs = (P(None, None, None, "freq"), P(None, None, None, "freq"), P(), P())
    out_specs = P(None, None, None, "freq")
    return jax.shard_map(
        per_device, mesh=mesh, in_specs=in_specs, out_specs=out_specs, check_vma=False
    )
```

profile of v0, /device:TPU:0, one launch (start us, length us, event | category | flops | bytes accessed | tf_op | source)
XLA Modules:
  0.0 1394.7 jit_solution(16185330490249208704)
XLA Ops:
  0.0 1.9 reshape.856
  2.8 1.8 reshape.893
  4.6 7.3 all-to-all-start
  12.1 14.9 %all-to-all-done = f32[32,1,3840]{2,1,0:T(1,128)S(1)} async-done(((f32[32,1,3840]{2,1,0:T(1,128)}), f32[32,1,3840]{2,1,0:T(1,128)S(1)}, u32[]{:S(2)}, u32[]{:S(2)}) %all-to-all-start) | async-done | bytes 491552 | tf_op jit(solution)/shard_map/all_to_all | solution.py:75
  27.6 1.8 reduce.20
  34.3 1.8 reshape.895
  36.1 3.1 all-to-all-start.1
  39.2 19.7 %fusion.344 = (f32[1,30,30,2048]{3,0,2,1:T(1,128)}, f32[1,30,30,2048]{3,0,2,1:T(1,128)}) fusion(f32[2,30,30,2048]{3,0,2,1:T(2,128)} %param.5), kind=kLoop, calls=%fused_computation.366 | loop fusion | bytes 29491200 | tf_op jit(solution)/shard_map/slice | solution.py:72
  60.3 1.8 reduce.21
  65.1 71.2 %fusion.12 = f32[30,2048]{1,0:T(8,128)S(1)} fusion(f32[1,1,30,2048]{3,1,2,0:T(1,128)S(1)} %get-tuple-element.41), kind=kOutput, calls=%fused_computation.15 | convolution fusion | flops 1572864000 | bytes 491520 | tf_op jit(solution)/shard_map/dot_general | solution.py:25
  136.3 71.4 %fusion.10 = f32[30,2048]{1,0:T(8,128)S(1)} fusion(f32[1,1,30,2048]{3,1,2,0:T(1,128)S(1)} %get-tuple-element.42), kind=kOutput, calls=%fused_computation.13 | convolution fusion | flops 1572864000 | bytes 491520 | tf_op jit(solution)/shard_map/dot_general | solution.py:28
  207.7 70.6 %fusion.65 = f32[2048,30]{0,1:T(8,128)S(1)} fusion(f32[30,2048]{1,0:T(8,128)S(1)} %fusion.12, f32[1,1,30,2048]{3,1,2,0:T(1,128)S(1)} %get-tuple-element.42), kind=kOutput, calls=%fused_computation.52 | convolution fusion | flops 1568731136 | bytes 737280 | tf_op jit(solution)/shard_map/dot_general | solution.py:25
  278.4 70.4 %fusion.71 = f32[2048,30]{0,1:T(8,128)S(1)} fusion(f32[30,2048]{1,0:T(8,128)S(1)} %fusion.10, f32[1,1,30,2048]{3,1,2,0:T(1,128)S(1)} %get-tuple-element.41), kind=kOutput, calls=%fused_computation.54 | convolution fusion | flops 1568731136 | bytes 737280 | tf_op jit(solution)/shard_map/dot_general | solution.py:28
  348.8 11.7 multiply_reduce_fusion.6
  361.2 1.3 copy.73
  362.5 1.4 copy.80
  364.0 6.9 fusion.100
  370.8 74.2 %fusion.30 = f32[30,2048]{1,0:T(8,128)S(1)} fusion(f32[30,2048]{0,1:T(8,128)S(1)} %get-tuple-element.21), kind=kOutput, calls=%fused_computation.28 | convolution fusion | flops 1568669696 | bytes 491520 | tf_op jit(solution)/shard_map/dot_general | solution.py:25
  445.1 74.4 %fusion.28 = f32[30,2048]{1,0:T(8,128)S(1)} fusion(f32[1,30,2048]{1,2,0:T(8,128)S(1)} %get-tuple-element.22), kind=kOutput, calls=%fused_computation.27 | convolution fusion | flops 1568669696 | bytes 491520 | tf_op jit(solution)/shard_map/dot_general | solution.py:28
  519.5 74.7 %fusion.50 = f32[30,2048]{1,0:T(8,128)S(1)} fusion(f32[30,2048]{1,0:T(8,128)S(1)} %fusion.30, f32[1,30,2048]{1,2,0:T(8,128)S(1)} %get-tuple-element.22), kind=kOutput, calls=%fused_computation.47 | convolution fusion | flops 1568731136 | bytes 737280 | tf_op jit(solution)/shard_map/dot_general | solution.py:25
  594.3 75.0 %multiply_subtract_fusion.2 = (f32[30,2048]{1,0:T(8,128)S(1)}, f32[30,2048]{1,0:T(8,128)S(1)}) fusion(f32[30,2048]{1,0:T(8,128)S(1)} %fusion.50, f32[2048]{0:T(1024)S(1)} %copy-done.12, f32[2048]{0:T(1024)S(1)} %copy-done.14, f32[30,2048]{1,0:T(8,128)S(1)} %fusion.28, f32[30,2048]{0,1:T(8,128)S(1)} %get-tuple-element.21), kind=kOutput, calls=%fused_computation.146 | convolution fusion | flops 1569099776 | bytes 1245184 | tf_op jit(solution)/shard_map/dot_general | solution.py:28
  670.9 1.4 pad_maximum_fusion
  674.3 20.9 %all_to_all.30 = f32[32,1,3840]{2,1,0:T(1,128)S(1)} all-to-all(f32[32,1,3840]{2,1,0:T(1,128)S(1)} %reshape.897), channel_id=1, replica_groups=mesh['freq'=32] {'freq'}, dimensions={0} | all-to-all | bytes 983040 | tf_op jit(solution)/shard_map/all_to_all | solution.py:106
  695.2 1.8 reduce.22
  701.3 2.1 fusion.107
  704.7 2.5 convolution_add_fusion.1
  707.3 2.6 subtract_bitcast_fusion
  711.8 17.7 %all_to_all.31 = f32[32,1,3840]{2,1,0:T(1,128)S(1)} all-to-all(f32[32,1,3840]{2,1,0:T(1,128)S(1)} %reshape.899), channel_id=1, replica_groups=mesh['freq'=32] {'freq'}, dimensions={0} | all-to-all | bytes 983040 | tf_op jit(solution)/shard_map/all_to_all | solution.py:81
  729.4 1.8 reduce.23
  734.2 71.6 %fusion.8 = f32[30,2048]{1,0:T(8,128)S(1)} fusion(f32[1,1,30,2048]{3,1,2,0:T(1,128)S(1)} %get-tuple-element.39), kind=kOutput, calls=%fused_computation.11 | convolution fusion | flops 1572864000 | bytes 491520 | tf_op jit(solution)/shard_map/dot_general | solution.py:25
  805.9 71.4 %fusion.6 = f32[30,2048]{1,0:T(8,128)S(1)} fusion(f32[1,1,30,2048]{3,1,2,0:T(1,128)S(1)} %get-tuple-element.40), kind=kOutput, calls=%fused_computation.9 | convolution fusion | flops 1572864000 | bytes 491520 | tf_op jit(solution)/shard_map/dot_general | solution.py:28
  877.3 70.4 %fusion.77 = f32[2048,30]{0,1:T(8,128)S(1)} fusion(f32[30,2048]{1,0:T(8,128)S(1)} %fusion.8, f32[1,1,30,2048]{3,1,2,0:T(1,128)S(1)} %get-tuple-element.40), kind=kOutput, calls=%fused_computation.56 | convolution fusion | flops 1568731136 | bytes 737280 | tf_op jit(solution)/shard_map/dot_general | solution.py:25
  947.7 70.6 %fusion.83 = f32[2048,30]{0,1:T(8,128)S(1)} fusion(f32[30,2048]{1,0:T(8,128)S(1)} %fusion.6, f32[1,1,30,2048]{3,1,2,0:T(1,128)S(1)} %get-tuple-element.39), kind=kOutput, calls=%fused_computation.58 | convolution fusion | flops 1568731136 | bytes 737280 | tf_op jit(solution)/shard_map/dot_general | solution.py:28
  1018.4 11.7 multiply_reduce_fusion.2
  1030.8 1.3 copy.87
  1032.1 1.3 copy.94
  1033.5 6.9 fusion.95
  1040.4 74.2 %fusion.22 = f32[30,2048]{1,0:T(8,128)S(1)} fusion(f32[30,2048]{0,1:T(8,128)S(1)} %get-tuple-element.19), kind=kOutput, calls=%fused_computation.24 | convolution fusion | flops 1568669696 | bytes 491520 | tf_op jit(solution)/shard_map/dot_general | solution.py:25
  1114.6 74.2 %fusion.20 = f32[30,2048]{1,0:T(8,128)S(1)} fusion(f32[1,30,2048]{1,2,0:T(8,128)S(1)} %get-tuple-element.20), kind=kOutput, calls=%fused_computation.23 | convolution fusion | flops 1568669696 | bytes 491520 | tf_op jit(solution)/shard_map/dot_general | solution.py:28
  1188.9 75.0 %fusion.56 = f32[30,2048]{1,0:T(8,128)S(1)} fusion(f32[30,2048]{1,0:T(8,128)S(1)} %fusion.22, f32[1,30,2048]{1,2,0:T(8,128)S(1)} %get-tuple-element.20), kind=kOutput, calls=%fused_computation.49 | convolution fusion | flops 1568731136 | bytes 737280 | tf_op jit(solution)/shard_map/dot_general | solution.py:25
  1263.9 74.8 %multiply_subtract_fusion.1 = (f32[30,2048]{1,0:T(8,128)S(1)}, f32[30,2048]{1,0:T(8,128)S(1)}) fusion(f32[30,2048]{1,0:T(8,128)S(1)} %fusion.56, f32[2048]{0:T(1024)S(1)} %copy-done.13, f32[2048]{0:T(1024)S(1)} %copy-done.15, f32[30,2048]{1,0:T(8,128)S(1)} %fusion.20, f32[30,2048]{0,1:T(8,128)S(1)} %get-tuple-element.19), kind=kOutput, calls=%fused_computation.144 | convolution fusion | flops 1569099776 | bytes 1245184 | tf_op jit(solution)/shard_map/dot_general | solution.py:28
  1340.2 1.4 pad_maximum_fusion.1
  1343.6 17.9 %all_to_all.32 = f32[32,1,3840]{2,1,0:T(1,128)S(1)} all-to-all(f32[32,1,3840]{2,1,0:T(1,128)S(1)} %reshape.901), channel_id=1, replica_groups=mesh['freq'=32] {'freq'}, dimensions={0} | all-to-all | bytes 983040 | tf_op jit(solution)/shard_map/all_to_all | solution.py:106
  1361.5 1.8 reduce.24
  1367.6 2.1 multiply_subtract_fusion
  1371.6 17.7 %all_to_all.33 = f32[32,1,3840]{2,1,0:T(1,128)S(1)} all-to-all(f32[32,1,3840]{2,1,0:T(1,128)S(1)} %reshape.903), channel_id=1, replica_groups=mesh['freq'=32] {'freq'}, dimensions={0} | all-to-all | bytes 983040 | tf_op jit(solution)/shard_map/all_to_all | solution.py:113
  1389.3 1.8 reduce.25
  1392.7 1.8 reshape.873
  (136 shorter events, 37.0 us)
Async XLA Ops:
  4.6 22.4 %all-to-all-start = ((f32[32,1,3840]{2,1,0:T(1,128)}), f32[32,1,3840]{2,1,0:T(1,128)S(1)}, u32[]{:S(2)}, u32[]{:S(2)}) async-start(f32[32,1,3840]{2,1,0:T(1,128)} %reshape.893), calls=%async_computation | async-start | bytes 983040 | tf_op jit(solution)/shard_map/all_to_all | solution.py:75
  12.1 46.8 %copy-start = (f32[64,32]{0,1:T(8,128)}, f32[64,32]{0,1:T(8,128)S(1)}, u32[]{:S(2)}) copy-start(f32[64,32]{0,1:T(8,128)S(1)} %get-tuple-element.46) | copy-start | bytes 24580
  12.1 46.8 %copy-start.2 = (f32[64,32]{0,1:T(8,128)}, f32[64,32]{0,1:T(8,128)S(1)}, u32[]{:S(2)}) copy-start(f32[64,32]{0,1:T(8,128)S(1)} %get-tuple-element.47) | copy-start | bytes 24580
  36.1 24.2 %all-to-all-start.1 = ((f32[32,1,3840]{2,1,0:T(1,128)}), f32[32,1,3840]{2,1,0:T(1,128)S(1)}, u32[]{:S(2)}, u32[]{:S(2)}) async-start(f32[32,1,3840]{2,1,0:T(1,128)} %reshape.895), calls=%async_computation.1 | async-start | bytes 983040 | tf_op jit(solution)/shard_map/all_to_all | solution.py:81
  39.2 21.0 %copy-start.24 = (f32[3,30]{1,0:T(4,128)S(1)}, f32[3,30]{1,0:T(4,128)}, u32[]{:S(2)}) copy-start(f32[3,30]{1,0:T(4,128)} %param.6) | copy-start | bytes 1084
  58.9 305.0 %copy-start.6 = (f32[2048]{0:T(1024)}, f32[2048]{0:T(1024)S(1)}, u32[]{:S(2)}) copy-start(f32[2048]{0:T(1024)S(1)} %fusion.202) | copy-start | bytes 24580
  58.9 289.8 %copy-start.4 = (f32[30,30]{1,0:T(8,128)}, f32[30,30]{1,0:T(8,128)S(1)}, u32[]{:S(2)}) copy-start(f32[30,30]{1,0:T(8,128)S(1)} %fusion.163) | copy-start | bytes 10804
  59.6 304.3 %copy-start.8 = (f32[2048]{0:T(1024)}, f32[2048]{0:T(1024)S(1)}, u32[]{:S(2)}) copy-start(f32[2048]{0:T(1024)S(1)} %get-tuple-element.48) | copy-start | bytes 24580
  60.3 303.7 %copy-start.10 = (f32[2048]{0:T(1024)}, f32[2048]{0:T(1024)S(1)}, u32[]{:S(2)}) copy-start(f32[2048]{0:T(1024)S(1)} %get-tuple-element.51) | copy-start | bytes 24580
  60.3 303.7 %copy-start.16 = (f32[30]{0:T(128)}, f32[30]{0:T(128)S(1)}, u32[]{:S(2)}) copy-start(f32[30]{0:T(128)S(1)} %get-tuple-element.43) | copy-start | bytes 364
  60.3 303.6 %copy-start.18 = (f32[30]{0:T(128)}, f32[30]{0:T(128)S(1)}, u32[]{:S(2)}) copy-start(f32[30]{0:T(128)S(1)} %get-tuple-element.44) | copy-start | bytes 364
  60.3 303.6 %copy-start.20 = (f32[30]{0:T(128)}, f32[30]{0:T(128)S(1)}, u32[]{:S(2)}) copy-start(f32[30]{0:T(128)S(1)} %get-tuple-element.45) | copy-start | bytes 364
  207.7 141.0 %slice-start = ((s8[7372800]{0:T(1024)(128)(4,1)}), s8[4194304]{0:T(1024)(128)(4,1)S(1)}, s32[]{:S(2)}) async-start(s8[7372800]{0:T(1024)(128)(4,1)} %bitcast.327), calls=%async_computation.6 | async-start | bytes 8388608
  207.7 141.0 %slice-start.4 = ((s8[7372800]{0:T(1024)(128)(4,1)}), s8[4194304]{0:T(1024)(128)(4,1)S(1)}, s32[]{:S(2)}) async-start(s8[7372800]{0:T(1024)(128)(4,1)} %bitcast.331), calls=%async_computation.10 | async-start | bytes 8388608
  278.3 70.4 %slice-start.1 = ((s8[7372800]{0:T(1024)(128)(4,1)}), s8[3178496]{0:T(1024)(128)(4,1)S(1)}, s32[]{:S(2)}) async-start(s8[7372800]{0:T(1024)(128)(4,1)} %bitcast.327), calls=%async_computation.7 | async-start | bytes 6356992
  278.4 70.4 %slice-start.5 = ((s8[7372800]{0:T(1024)(128)(4,1)}), s8[3178496]{0:T(1024)(128)(4,1)S(1)}, s32[]{:S(2)}) async-start(s8[7372800]{0:T(1024)(128)(4,1)} %bitcast.331), calls=%async_computation.11 | async-start | bytes 6356992
  519.5 74.8 %copy-start.12 = (f32[2048]{0:T(1024)S(1)}, f32[2048]{0:T(1024)}, u32[]{:S(2)}) copy-start(f32[2048]{0:T(1024)} %get-tuple-element.49) | copy-start | bytes 24580
  519.5 74.8 %copy-start.14 = (f32[2048]{0:T(1024)S(1)}, f32[2048]{0:T(1024)}, u32[]{:S(2)}) copy-start(f32[2048]{0:T(1024)} %get-tuple-element.50) | copy-start | bytes 24580
  669.3 32.0 %copy-start.22 = (f32[30]{0:T(128)S(1)}, f32[30]{0:T(128)}, u32[]{:S(2)}) copy-start(f32[30]{0:T(128)} %param.7) | copy-start | bytes 364
  669.3 37.9 %copy-start.1 = (f32[64,32]{0,1:T(8,128)S(1)}, f32[64,32]{0,1:T(8,128)}, u32[]{:S(2)}) copy-start(f32[64,32]{0,1:T(8,128)} %copy-done) | copy-start | bytes 24580
  669.3 37.9 %copy-start.3 = (f32[64,32]{0,1:T(8,128)S(1)}, f32[64,32]{0,1:T(8,128)}, u32[]{:S(2)}) copy-start(f32[64,32]{0,1:T(8,128)} %copy-done.2) | copy-start | bytes 24580
  805.8 212.4 %slice-start.2 = ((s8[7372800]{0:T(1024)(128)(4,1)}), s8[4194304]{0:T(1024)(128)(4,1)S(1)}, s32[]{:S(2)}) async-start(s8[7372800]{0:T(1024)(128)(4,1)} %bitcast.329), calls=%async_computation.8 | async-start | bytes 8388608
  805.8 212.4 %slice-start.6 = ((s8[7372800]{0:T(1024)(128)(4,1)}), s8[4194304]{0:T(1024)(128)(4,1)S(1)}, s32[]{:S(2)}) async-start(s8[7372800]{0:T(1024)(128)(4,1)} %bitcast.333), calls=%async_computation.12 | async-start | bytes 8388608
  877.2 141.1 %slice-start.3 = ((s8[7372800]{0:T(1024)(128)(4,1)}), s8[3178496]{0:T(1024)(128)(4,1)S(1)}, s32[]{:S(2)}) async-start(s8[7372800]{0:T(1024)(128)(4,1)} %bitcast.329), calls=%async_computation.9 | async-start | bytes 6356992
  877.2 141.1 %slice-start.7 = ((s8[7372800]{0:T(1024)(128)(4,1)}), s8[3178496]{0:T(1024)(128)(4,1)S(1)}, s32[]{:S(2)}) async-start(s8[7372800]{0:T(1024)(128)(4,1)} %bitcast.333), calls=%async_computation.13 | async-start | bytes 6356992
  947.7 70.7 %copy-start.5 = (f32[30,30]{1,0:T(8,128)S(1)}, f32[30,30]{1,0:T(8,128)}, u32[]{:S(2)}) copy-start(f32[30,30]{1,0:T(8,128)} %copy-done.4) | copy-start | bytes 10804
  1018.3 15.2 %copy-start.7 = (f32[2048]{0:T(1024)S(1)}, f32[2048]{0:T(1024)}, u32[]{:S(2)}) copy-start(f32[2048]{0:T(1024)} %copy-done.6) | copy-start | bytes 24580
  1018.4 15.1 %copy-start.9 = (f32[2048]{0:T(1024)S(1)}, f32[2048]{0:T(1024)}, u32[]{:S(2)}) copy-start(f32[2048]{0:T(1024)} %copy-done.8) | copy-start | bytes 24580
  1018.4 15.1 %copy-start.11 = (f32[2048]{0:T(1024)S(1)}, f32[2048]{0:T(1024)}, u32[]{:S(2)}) copy-start(f32[2048]{0:T(1024)} %copy-done.10) | copy-start | bytes 24580
  1018.4 15.1 %copy-start.17 = (f32[30]{0:T(128)S(1)}, f32[30]{0:T(128)}, u32[]{:S(2)}) copy-start(f32[30]{0:T(128)} %copy-done.16) | copy-start | bytes 364
  1018.4 15.1 %copy-start.19 = (f32[30]{0:T(128)S(1)}, f32[30]{0:T(128)}, u32[]{:S(2)}) copy-start(f32[30]{0:T(128)} %copy-done.18) | copy-start | bytes 364
  1018.4 15.1 %copy-start.21 = (f32[30]{0:T(128)S(1)}, f32[30]{0:T(128)}, u32[]{:S(2)}) copy-start(f32[30]{0:T(128)} %copy-done.20) | copy-start | bytes 364
  1188.8 75.0 %copy-start.13 = (f32[2048]{0:T(1024)S(1)}, f32[2048]{0:T(1024)}, u32[]{:S(2)}) copy-start(f32[2048]{0:T(1024)} %get-tuple-element.49) | copy-start | bytes 24580
  1188.9 75.0 %copy-start.15 = (f32[2048]{0:T(1024)S(1)}, f32[2048]{0:T(1024)}, u32[]{:S(2)}) copy-start(f32[2048]{0:T(1024)} %get-tuple-element.50) | copy-start | bytes 24580
  1338.6 29.0 %copy-start.23 = (f32[30]{0:T(128)S(1)}, f32[30]{0:T(128)}, u32[]{:S(2)}) copy-start(f32[30]{0:T(128)} %param.7) | copy-start | bytes 364
where the time goes:
time: 1400 us; the launch traced here: 1390 us
  matrix products  1180 us (84%)
  blocking collectives  74.2 us (5%)
  local copies, waits for them, and re-layouts  58.3 us (4%)
  other arithmetic  57.4 us (4%)
  waiting for transfers between devices  14.9 us (1%)
    dot_general x8, matrix products, transform(): jnp.matmul(imag_part, sine, precision=HIGHEST)  297 us
    dot_general x8, matrix products, transform(): jnp.matmul(real_part, sine, precision=HIGHEST)  295 us
    dot_general x8, matrix products, transform(): jnp.matmul(imag_part, cosine, precision=HIGHEST)  294 us
    dot_general x8, matrix products, transform(): jnp.matmul(real_part, cosine, precision=HIGHEST)  292 us
    all_to_all x2, blocking collectives, per_device(): lax.all_to_all(moved, 'freq', split_axis=4, concat_axis=4, tiled=True)  38.8 us
  transfers between devices with their start and end apart: 2, of which 1 were waited for; matrix products, arithmetic and copies ran while one was open for 2% of the time, Pallas kernels for 0%

commit v1 on v0

--- a/solution.py
+++ b/solution.py
@@ -1,6 +1,11 @@
+import functools
+
 import jax
 import jax.numpy as jnp
+import numpy as np
 from jax import lax
+from jax.experimental import pallas as pl
+from jax.experimental.pallas import tpu as pltpu
 from jax.sharding import PartitionSpec as P
 
 STEPS = 2
@@ -114,9 +119,403 @@
     return returned.reshape(columns.shape[0], 2, mode_count, local_count)
 
 
+LANES = 128
+HALF = LANES // 2
+SUB = 8
+
+
+def low_lanes(shape):
+    return lax.broadcasted_iota(jnp.int32, shape, len(shape) - 1) < HALF
+
+
+def swap(x):
+    return pltpu.roll(x, HALF, 1)
+
+
+def sign_row(rows):
+    return jnp.where(low_lanes((rows, LANES)), -1.0, 1.0).astype(jnp.float32)
+
+
+def times_root(x, index, count, orient, sgn):
+    eighth = 8 * index
+    if index == 0:
+        return x
+    if eighth == 2 * count:
+        return swap(x) * (sgn * orient)
+    angle = 2.0 * np.pi * index / count
+    return x * float(np.cos(angle)) + swap(x) * (sgn * float(orient * np.sin(angle)))
+
+
+def short_fft(items, orient, sgn):
+    count = len(items)
+    if count == 1:
+        return items
+    even = short_fft(items[0::2], orient, sgn)
+    odd = short_fft(items[1::2], orient, sgn)
+    turned = [times_root(v, k, count, orient, sgn) for k, v in enumerate(odd)]
+    return [e + t for e, t in zip(even, turned)] + [e - t for e, t in zip(even, turned)]
+
+
+def packed_mul(x, cosine, signed_sine):
+    return x * cosine + swap(x) * signed_sine
+
+
+def split_constant(value, pieces, bits):
+    parts = []
+    for _ in range(pieces - 1):
+        exponent = np.floor(np.log2(value))
+        unit = 2.0 ** (exponent - bits + 1)
+        part = np.floor(value / unit) * unit
+        parts.append(float(part))
+        value -= part
+    return parts + [float(value)]
+
+
+HALF_PI = split_constant(np.pi / 2, 4, 8)
+
+
+def sine_cosine(theta):
+    turns = jnp.floor(theta * float(2 / np.pi) + 0.5)
+    rest = theta
+    for part in HALF_PI:
+        rest = rest - turns * part
+    square = rest * rest
+    sine = rest + rest * square * (
+        -1.6666654611e-1 + square * (8.3321608736e-3 - square * 1.9515295891e-4)
+    )
+    cosine = 1.0 - 0.5 * square + square * square * (
+        4.166664568298827e-2 + square * (-1.388731625493765e-3 + square * 2.443315711809948e-5)
+    )
+    quadrant = turns.astype(jnp.int32) & 3
+    crossed = (quadrant & 1) == 1
+    out_sine = jnp.where(crossed, cosine, sine)
+    out_cosine = jnp.where(crossed, sine, cosine)
+    out_sine = jnp.where(quadrant >= 2, -out_sine, out_sine)
+    out_cosine = jnp.where((quadrant == 1) | (quadrant == 2), -out_cosine, out_cosine)
+    return out_sine, out_cosine
+
+
+def exchange_kernel(count, x_ref, out_ref, send_sem, recv_sem, local_sem):
+    me = lax.axis_index("freq")
+    barrier = pltpu.get_barrier_semaphore()
+
+    def greet(k, carry):
+        pl.semaphore_signal(
+            barrier, inc=1, device_id=((me + k) % count,), device_id_type=pl.DeviceIdType.MESH
+        )
+        return carry
+
+    lax.fori_loop(1, count, greet, 0)
+    own = pltpu.make_async_copy(x_ref.at[me], out_ref.at[me], local_sem)
+    own.start()
+    pl.semaphore_wait(barrier, count - 1)
+
+    def copy(k, slot):
+        peer = (me + k) % count
+        return pltpu.make_async_remote_copy(
+            src_ref=x_ref.at[peer],
+            dst_ref=out_ref.at[slot],
+            send_sem=send_sem.at[k],
+            recv_sem=recv_sem.at[k],
+            device_id=(peer,),
+            device_id_type=pl.DeviceIdType.MESH,
+        )
+
+    def send(k, carry):
+        copy(k, me).start()
+        return carry
+
+    def drain(k, carry):
+        copy(k, (me - k + count) % count).wait_recv()
+        return carry
+
+    def finish(k, carry):
+        copy(k, me).wait_send()
+        return carry
+
+    lax.fori_loop(1, count, send, 0)
+    own.wait()
+    lax.fori_loop(1, count, drain, 0)
+    lax.fori_loop(1, count, finish, 0)
+
+
+def exchange(x):
+    count = x.shape[0]
+    return pl.pallas_call(
+        functools.partial(exchange_kernel, count),
+        out_shape=jax.ShapeDtypeStruct(x.shape, x.dtype),
+        in_specs=[pl.BlockSpec(memory_space=pltpu.VMEM)],
+        out_specs=pl.BlockSpec(memory_space=pltpu.VMEM),
+        scratch_shapes=[
+            pltpu.SemaphoreType.DMA((count,)),
+            pltpu.SemaphoreType.DMA((count,)),
+            pltpu.SemaphoreType.DMA(()),
+        ],
+        compiler_params=pltpu.CompilerParams(collective_id=0, has_side_effects=True),
+        name="exchange",
+    )(x)
+
+
+def column_kernel(inverse, forward, scale, x_ref, cos_ref, sin_ref, gain_ref, out_ref, field):
+    count, rows = x_ref.shape[0], x_ref.shape[1]
+    sgn = sign_row(SUB)
+
+    def chunk(c):
+        return pl.ds(pl.multiple_of(c * SUB, SUB), SUB)
+
+    if inverse:
+
+        def undo(c, carry):
+            rows_of = chunk(c)
+            items = [
+                packed_mul(
+                    x_ref[d, rows_of, :], cos_ref[d : d + 1, :] * scale, sin_ref[d : d + 1, :] * -scale
+                )
+                for d in range(count)
+            ]
+            for a, value in enumerate(short_fft(items, 1.0, sgn)):
+                field[a, rows_of, :] = value
+            return carry
+
+        lax.fori_loop(0, rows // SUB, undo, 0)
+        wide = sign_row(rows)
+        target = field if forward else out_ref
+
+        def kerr(a, carry):
+            x = field[a]
+            square = x * x
+            magnitude = square + swap(square)
+            power = jnp.sum(magnitude, axis=0, keepdims=True)
+            sine, cosine = sine_cosine(gain_ref[...] * (2.0 * power - magnitude))
+            target[a] = packed_mul(x, cosine, sine * wide)
+            return carry
+
+        lax.fori_loop(0, count, kerr, 0, unroll=2)
+    if forward:
+        source = field if inverse else x_ref
+
+        def apply(c, carry):
+            rows_of = chunk(c)
+            items = short_fft([source[a, rows_of, :] for a in range(count)], -1.0, sgn)
+            for d, value in enumerate(items):
+                out_ref[d, rows_of, :] = packed_mul(value, cos_ref[d : d + 1, :], sin_ref[d : d + 1, :])
+            return carry
+
+        lax.fori_loop(0, rows // SUB, apply, 0)
+
+
+def column_stage(x, twist_cos, twist_sin, gain, scale, inverse, forward):
+    return pl.pallas_call(
+        functools.partial(column_kernel, inverse, forward, scale),
+        out_shape=jax.ShapeDtypeStruct(x.shape, x.dtype),
+        in_specs=[pl.BlockSpec(memory_space=pltpu.VMEM)] * 4,
+        out_specs=pl.BlockSpec(memory_space=pltpu.VMEM),
+        scratch_shapes=[pltpu.VMEM(x.shape, jnp.float32)],
+        name="column",
+    )(x, twist_cos, twist_sin, gain)
+
+
+def long_dft(x, weights):
+    high = x.astype(jnp.bfloat16)
+    low = (x - high.astype(jnp.float32)).astype(jnp.bfloat16)
+    both = jnp.concatenate((high, low), axis=1)
+    product = jnp.dot(both, weights, preferred_element_type=jnp.float32)
+    return product[:, :LANES] + product[:, LANES:]
+
+
+def row_kernel(
+    x_ref, c_ref, spread_cos_ref, spread_sin_ref, tw_cos_ref, tw_sin_ref, fwd_ref, inv_ref,
+    out_ref, spec, mixed, sum_real, sum_imag,
+):
+    tile = pl.program_id(0)
+    count, rows = x_ref.shape[0], x_ref.shape[1]
+    modes = c_ref.shape[1]
+    sgn = sign_row(SUB)
+
+    def chunk(c):
+        return pl.ds(pl.multiple_of(c * SUB, SUB), SUB)
+
+    @pl.when(tile == 0)
+    def _():
+        sum_real[...] = jnp.zeros_like(sum_real)
+        sum_imag[...] = jnp.zeros_like(sum_imag)
+
+        def lanes(q, carry):
+            part = pl.ds(q * 4, 4)
+            block = x_ref[part].reshape(4 * rows, LANES)
+            spec[part] = long_dft(block, fwd_ref[...]).reshape(4, rows, LANES)
+            return carry
+
+        lax.fori_loop(0, count // 4, lanes, 0)
+
+        def across(c, carry):
+            rows_of = chunk(c)
+            items = [
+                packed_mul(spec[p, rows_of, :], tw_cos_ref[p : p + 1, :], tw_sin_ref[p : p + 1, :])
+                for p in range(count)
+            ]
+            for j, value in enumerate(short_fft(items, -1.0, sgn)):
+                spec[j, rows_of, :] = value
+            return carry
+
+        lax.fori_loop(0, rows // SUB, across, 0)
+
+    first, second = spec[2 * tile], spec[2 * tile + 1]
+    low = low_lanes((rows, LANES))
+    real = jnp.where(low, first, swap(second))
+    imag = jnp.where(low, swap(first), second)
+    real_part, imag_part = real[:modes], imag[:modes]
+    for n in range(modes):
+        coup_real, coup_imag = c_ref[0, n], c_ref[1, n]
+        sum_real[n : n + 1, :] = jnp.sum(
+            coup_real * real_part - coup_imag * imag_part, axis=0, keepdims=True
+        )
+        sum_imag[n : n + 1, :] = jnp.sum(
+            coup_real * imag_part + coup_imag * real_part, axis=0, keepdims=True
+        )
+    total_real, total_imag = sum_real[...] + real, sum_imag[...] + imag
+    total_real, total_imag = rotate(
+        total_real, total_imag, spread_cos_ref[...], spread_sin_ref[...]
+    )
+    mixed[2 * tile] = jnp.where(low, total_real, swap(total_imag))
+    mixed[2 * tile + 1] = jnp.where(low, swap(total_real), total_imag)
+
+    @pl.when(tile == pl.num_programs(0) - 1)
+    def _():
+        def across(c, carry):
+            rows_of = chunk(c)
+            items = short_fft([mixed[j, rows_of, :] for j in range(count)], 1.0, sgn)
+            for p, value in enumerate(items):
+                mixed[p, rows_of, :] = packed_mul(
+                    value, tw_cos_ref[p : p + 1, :], -tw_sin_ref[p : p + 1, :]
+                )
+            return carry
+
+        lax.fori_loop(0, rows // SUB, across, 0)
+
+        def lanes(q, carry):
+            part = pl.ds(q * 4, 4)
+            block = mixed[part].reshape(4 * rows, LANES)
+            out_ref[part] = long_dft(block, inv_ref[...]).reshape(4, rows, LANES)
+            return carry
+
+        lax.fori_loop(0, count // 4, lanes, 0)
+
+
+def row_stage(x, coupling, spread_cos, spread_sin, tw_cos, tw_sin, fwd, inv):
+    rows = x.shape[1]
+    modes = coupling.shape[1]
+    tiles = coupling.shape[3] // LANES
+    whole = lambda array: pl.BlockSpec(array.shape, lambda t: (0,) * array.ndim)
+    return pl.pallas_call(
+        row_kernel,
+        grid=(tiles,),
+        out_shape=jax.ShapeDtypeStruct(x.shape, x.dtype),
+        in_specs=[
+            whole(x),
+            pl.BlockSpec((2, modes, modes, LANES), lambda t: (0, 0, 0, t)),
+            pl.BlockSpec((rows, LANES), lambda t: (0, t)),
+            pl.BlockSpec((rows, LANES), lambda t: (0, t)),
+            whole(tw_cos),
+            whole(tw_sin),
+            whole(fwd),
+            whole(inv),
+        ],
+        out_specs=whole(x),
+        scratch_shapes=[
+            pltpu.VMEM(x.shape, jnp.float32),
+            pltpu.VMEM(x.shape, jnp.float32),
+            pltpu.VMEM((rows, LANES), jnp.float32),
+            pltpu.VMEM((rows, LANES), jnp.float32),
+        ],
+        compiler_params=pltpu.CompilerParams(dimension_semantics=("arbitrary",)),
+        name="row",
+    )(x, coupling, spread_cos, spread_sin, tw_cos, tw_sin, fwd, inv)
+
+
+def packed_table(cosine, sine):
+    xp = np if isinstance(cosine, np.ndarray) else jnp
+    return (
+        xp.concatenate((cosine, cosine), axis=1).astype(xp.float32),
+        xp.concatenate((-sine, sine), axis=1).astype(xp.float32),
+    )
+
+
+def dft_weights(size, orient):
+    index = np.arange(size)
+    angle = orient * 2.0 * np.pi * (index[:, None] * index[None, :] % size) / size
+    cosine, sine = np.cos(angle), np.sin(angle)
+    full = np.block([[cosine, sine], [-sine, cosine]]).astype(np.float32)
+    high = full.astype(jnp.bfloat16)
+    low = (full - high.astype(np.float32)).astype(jnp.bfloat16)
+    return np.block([[high, low], [high, np.zeros_like(low)]])
+
+
+def packed_device(pulses, coupling, dispersion_terms, kerr_gain):
+    shards = lax.axis_size("freq")
+    device = lax.axis_index("freq")
+    modes, local = pulses.shape[2], pulses.shape[3]
+    groups = local // shards
+    total = local * shards
+    rows = -(-modes // SUB) * SUB
+    pad = rows - modes
+
+    shard_index = np.arange(shards)
+    angle = -2.0 * np.pi * (shard_index[:, None] * np.arange(groups)[None, :] % local) / local
+    tw_cos, tw_sin = packed_table(np.cos(angle), np.sin(angle))
+    fwd, inv = dft_weights(groups, -1.0), dft_weights(groups, 1.0)
+    samples = device + shards * jnp.arange(groups, dtype=jnp.int32)
+    twist_cos, twist_sin = packed_table(
+        *angle_table(jnp.arange(shards, dtype=jnp.int32), samples, total, -1.0)
+    )
+    gain = jnp.broadcast_to(jnp.pad(kerr_gain, (0, pad))[:, None], (rows, LANES))
+
+    bins = device + shards * jnp.arange(local, dtype=jnp.int32)
+    signed_bin = jnp.where(bins < total // 2, bins, bins - total).astype(jnp.float32)
+    angular = signed_bin / (total // 2)
+    terms = jnp.pad(dispersion_terms, ((0, 0), (0, pad)))
+    dispersion = (
+        terms[0][:, None] * angular
+        + terms[1][:, None] * angular**2 / 2
+        + terms[2][:, None] * angular**3 / 6
+    )
+    spread_cos, spread_sin = jnp.cos(dispersion), jnp.sin(dispersion)
+
+    blocks = pulses.reshape(2, modes, groups, shards).transpose(3, 1, 0, 2)
+    x = jnp.pad(blocks.reshape(shards, modes, 2 * groups), ((0, 0), (0, pad), (0, 0)))
+    scale = 1.0 / total
+    for repeat in range(STEPS):
+        x = exchange(x) if repeat == 0 else x
+        if repeat == 0:
+            x = column_stage(x, twist_cos, twist_sin, gain, scale, False, True)
+        x = exchange(x)
+        x = row_stage(x, coupling, spread_cos, spread_sin, tw_cos, tw_sin, fwd, inv)
+        x = exchange(x)
+        x = column_stage(x, twist_cos, twist_sin, gain, scale, True, repeat < STEPS - 1)
+    x = exchange(x)
+    x = x[:, :modes].reshape(shards, modes, 2, groups).transpose(2, 1, 3, 0)
+    return x.reshape(1, 2, modes, local)
+
+
+def fits(shards, pulses):
+    local = pulses.shape[3] // shards
+    return (
+        pulses.shape[0] == 1
+        and shards & (shards - 1) == 0
+        and shards >= 4
+        and local == shards * HALF
+    )
+
+
 def solution(mesh):
     in_specs = (P(None, None, None, "freq"), P(None, None, None, "freq"), P(), P())
     out_specs = P(None, None, None, "freq")
-    return jax.shard_map(
-        per_device, mesh=mesh, in_specs=in_specs, out_specs=out_specs, check_vma=False
-    )
+    shards = mesh.shape["freq"]
+
+    def run(pulses, coupling, dispersion_terms, kerr_gain):
+        body = packed_device if fits(shards, pulses) else per_device
+        return jax.shard_map(
+            body, mesh=mesh, in_specs=in_specs, out_specs=out_specs, check_vma=False
+        )(pulses, coupling, dispersion_terms, kerr_gain)
+
+    return run

time: 1400 us -> 207 us (0.15)
  matrix products: 1180 us -> 0 us
  Pallas kernels: 0 us -> 173 us
  blocking collectives: 74.2 us -> 0 us
  other arithmetic: 57.4 us -> 2.65 us
  local copies, waits for them, and re-layouts: 58.3 us -> 29.4 us
  waiting for transfers between devices: 14.9 us -> 0 us
    dot_general x32 -> x0, matrix products: 1180 us -> none  [the longest x8 297 us: transform(): jnp.matmul(imag_part, sine, precision=HIGHEST)]
    pallas_call x0 -> x11, Pallas kernels: none -> 173 us  [the longest x6 115 us: exchange(): pl.pallas_call(functools.partial(exchange_kernel, count), out_shape=jax.S...]
    all_to_all x4 -> x0, blocking collectives: 74.2 us -> none  [the longest x2 38.8 us: per_device(): lax.all_to_all(moved, 'freq', split_axis=4, concat_axis=4, tiled=True)]
    unnamed x6 -> x0, other arithmetic: 23.4 us -> none
    slice x7 -> x1, local copies, waits for them, and re-layouts: 22.7 us -> 1.33 us  [packed_device(): x = x[:, :modes].reshape(shards, modes, 2, groups).transpose(2, 1, 3, 0)]
    another operation x7 -> x0, other arithmetic: 16.8 us -> none
    all_to_all x2 -> x0, waiting for transfers between devices: 14.9 us -> none  [the longest x1 14.9 us: per_device(): lax.all_to_all(blocks, 'freq', split_axis=4, concat_axis=4, tiled=True)]
  transfers between devices with their start and end apart: 2 -> 0, of which waited for: 1 -> 0; matrix products, arithmetic and copies ran while one was open for 2% -> 0% of each run, Pallas kernels for 0% -> 0%
where the time goes in v1:
time: 207 us; the launch traced here: 205 us
  Pallas kernels  173 us (84%)
  local copies, waits for them, and re-layouts  29.4 us (14%)
  other arithmetic  2.65 us (1%)
    pallas_call x6, Pallas kernels, exchange(): pl.pallas_call(functools.partial(exchange_kernel, count), out_shape=jax.S...  115 us
    pallas_call x2, Pallas kernels, row_stage(): pl.pallas_call(row_kernel, grid=(tiles,), out_shape=jax.ShapeDtypeStruct(...  40.7 us
    unnamed x1, local copies, waits for them, and re-layouts  19.3 us
    pallas_call x3, Pallas kernels, column_stage(): pl.pallas_call(functools.partial(column_kernel, inverse, forward, scale),...  16.6 us

profile of v1, /device:TPU:0, one launch (start us, length us, event | category | flops | bytes accessed | tf_op | source)
XLA Modules:
  0.0 204.6 jit_solution(5286107238629375440)
XLA Ops:
  0.0 0.7 pad.13
  0.7 0.8 fusion.14
  1.5 0.7 broadcast_in_dim.2.gain_ref
  2.2 0.1 fusion.11
  2.2 0.7 pad_maximum_fusion
  2.9 1.8 fusion
  4.8 1.9 reshape.37
  6.7 0.7 copy.14
  7.4 0.8 pad.12.x_ref
  8.2 18.4 %exchange.6.x_ref = f32[32,32,128]{2,1,0:T(8,128)} custom-call(f32[32,32,128]{2,1,0:T(8,128)} %pad.12.x_ref), custom_call_target="tpu_custom_call" | custom-call | tf_op jit(solution)/shard_map/exchange/pallas_call | solution.py:244
  26.6 3.5 %column.3.x_ref = f32[32,32,128]{2,1,0:T(8,128)} custom-call(f32[32,32,128]{2,1,0:T(8,128)} %exchange.6.x_ref, f32[32,128]{1,0:T(8,128)} %get-tuple-element.15.cos_ref, f32[32,128]{1,0:T(8,128)} %get-tuple-element.16.sin_ref, f32[32,128]{1,0:T(8,128)} %broadcast_in_dim.2.gain_ref), custom_call_target="tpu_custom_call" | custom-call | tf_op jit(solution)/shard_map/column/pallas_call | solution.py:308
  30.1 19.4 %exchange.7.x_ref = f32[32,32,128]{2,1,0:T(8,128)} custom-call(f32[32,32,128]{2,1,0:T(8,128)} %column.3.x_ref), custom_call_target="tpu_custom_call" | custom-call | tf_op jit(solution)/shard_map/exchange/pallas_call | solution.py:244
  49.5 19.3 %copy.15.c_ref = f32[2,30,30,2048]{3,2,1,0:T(8,128)} copy(f32[2,30,30,2048]{3,0,2,1:T(2,128)} %param.9) | data formatting | bytes 29491200 | tf_op args[1]
  68.8 20.3 %row.2.x_ref = f32[32,32,128]{2,1,0:T(8,128)} custom-call(f32[32,32,128]{2,1,0:T(8,128)} %exchange.7.x_ref, f32[2,30,30,2048]{3,2,1,0:T(8,128)} %copy.15.c_ref, f32[32,2048]{1,0:T(8,128)} %get-tuple-element.6.spread_cos_ref, f32[32,2048]{1,0:T(8,128)} %get-tuple-element.5.spread_sin_ref, f32[32,128]{1,0:T(8,128)} %constant.51.clone.tw_cos_ref, ...), custom_call_target="tpu_custom_call" | custom-call | tf_op jit(solution)/shard_map/row/pallas_call | solution.py:410
  89.1 19.4 %exchange.8.x_ref = f32[32,32,128]{2,1,0:T(8,128)} custom-call(f32[32,32,128]{2,1,0:T(8,128)} %row.2.x_ref), custom_call_target="tpu_custom_call" | custom-call | tf_op jit(solution)/shard_map/exchange/pallas_call | solution.py:244
  108.5 7.4 %column.4.x_ref = f32[32,32,128]{2,1,0:T(8,128)} custom-call(f32[32,32,128]{2,1,0:T(8,128)} %exchange.8.x_ref, f32[32,128]{1,0:T(8,128)} %get-tuple-element.15.cos_ref, f32[32,128]{1,0:T(8,128)} %get-tuple-element.16.sin_ref, f32[32,128]{1,0:T(8,128)} %broadcast_in_dim.2.gain_ref), custom_call_target="tpu_custom_call" | custom-call | tf_op jit(solution)/shard_map/column/pallas_call | solution.py:308
  115.8 19.4 %exchange.9.x_ref = f32[32,32,128]{2,1,0:T(8,128)} custom-call(f32[32,32,128]{2,1,0:T(8,128)} %column.4.x_ref), custom_call_target="tpu_custom_call" | custom-call | tf_op jit(solution)/shard_map/exchange/pallas_call | solution.py:244
  135.2 20.4 %row.3.x_ref = f32[32,32,128]{2,1,0:T(8,128)} custom-call(f32[32,32,128]{2,1,0:T(8,128)} %exchange.9.x_ref, f32[2,30,30,2048]{3,2,1,0:T(8,128)} %copy.15.c_ref, f32[32,2048]{1,0:T(8,128)} %get-tuple-element.6.spread_cos_ref, f32[32,2048]{1,0:T(8,128)} %get-tuple-element.5.spread_sin_ref, f32[32,128]{1,0:T(8,128)} %constant.51.clone.tw_cos_ref, ...), custom_call_target="tpu_custom_call" | custom-call | tf_op jit(solution)/shard_map/row/pallas_call | solution.py:410
  155.6 19.4 %exchange.10.x_ref = f32[32,32,128]{2,1,0:T(8,128)} custom-call(f32[32,32,128]{2,1,0:T(8,128)} %row.3.x_ref), custom_call_target="tpu_custom_call" | custom-call | tf_op jit(solution)/shard_map/exchange/pallas_call | solution.py:244
  175.0 5.7 %column.5.x_ref = f32[32,32,128]{2,1,0:T(8,128)} custom-call(f32[32,32,128]{2,1,0:T(8,128)} %exchange.10.x_ref, f32[32,128]{1,0:T(8,128)} %get-tuple-element.15.cos_ref, f32[32,128]{1,0:T(8,128)} %get-tuple-element.16.sin_ref, f32[32,128]{1,0:T(8,128)} %broadcast_in_dim.2.gain_ref), custom_call_target="tpu_custom_call" | custom-call | tf_op jit(solution)/shard_map/column/pallas_call | solution.py:308
  180.7 19.4 %exchange.11 = f32[32,32,128]{2,1,0:T(8,128)} custom-call(f32[32,32,128]{2,1,0:T(8,128)} %column.5.x_ref), custom_call_target="tpu_custom_call" | custom-call | tf_op jit(solution)/shard_map/exchange/pallas_call | solution.py:244
  200.1 1.3 copy.17
  201.4 0.6 reshape.39
  202.0 0.8 copy.18
  202.8 1.8 reshape.40
  (3 shorter events, 0.0 us)

commit v2 on v1

--- a/solution.py
+++ b/solution.py
@@ -195,9 +195,13 @@
     return out_sine, out_cosine
 
 
-def exchange_kernel(count, x_ref, out_ref, send_sem, recv_sem, local_sem):
+def exchange_kernel(count, modes, x_ref, out_ref, send_sem, recv_sem, local_sem):
     me = lax.axis_index("freq")
     barrier = pltpu.get_barrier_semaphore()
+    rows = x_ref.shape[1]
+    if rows > modes:
+        spare = pl.ds(rows - SUB, SUB)
+        out_ref[:, spare, :] = jnp.zeros((count, SUB, x_ref.shape[2]), x_ref.dtype)
 
     def greet(k, carry):
         pl.semaphore_signal(
@@ -206,23 +210,25 @@
         return carry
 
     lax.fori_loop(1, count, greet, 0)
-    own = pltpu.make_async_copy(x_ref.at[me], out_ref.at[me], local_sem)
+    own = pltpu.make_async_copy(
+        x_ref.at[me, pl.ds(0, modes)], out_ref.at[me, pl.ds(0, modes)], local_sem
+    )
     own.start()
     pl.semaphore_wait(barrier, count - 1)
 
     def copy(k, slot):
         peer = (me + k) % count
         return pltpu.make_async_remote_copy(
-            src_ref=x_ref.at[peer],
-            dst_ref=out_ref.at[slot],
+            src_ref=x_ref.at[peer, pl.ds(0, modes)],
+            dst_ref=out_ref.at[slot, pl.ds(0, modes)],
             send_sem=send_sem.at[k],
             recv_sem=recv_sem.at[k],
             device_id=(peer,),
             device_id_type=pl.DeviceIdType.MESH,
         )
 
-    def send(k, carry):
-        copy(k, me).start()
+    def send(j, carry):
+        copy(count // 2 + (j // 2) * (1 - 2 * (j % 2)), me).start()
         return carry
 
     def drain(k, carry):
@@ -239,10 +245,10 @@
     lax.fori_loop(1, count, finish, 0)
 
 
-def exchange(x):
+def exchange(x, modes):
     count = x.shape[0]
     return pl.pallas_call(
-        functools.partial(exchange_kernel, count),
+        functools.partial(exchange_kernel, count, modes),
         out_shape=jax.ShapeDtypeStruct(x.shape, x.dtype),
         in_specs=[pl.BlockSpec(memory_space=pltpu.VMEM)],
         out_specs=pl.BlockSpec(memory_space=pltpu.VMEM),
@@ -325,20 +331,20 @@
 
 def row_kernel(
     x_ref, c_ref, spread_cos_ref, spread_sin_ref, tw_cos_ref, tw_sin_ref, fwd_ref, inv_ref,
-    out_ref, spec, mixed, sum_real, sum_imag,
+    out_ref, spec, by_real, by_imag, total,
 ):
-    tile = pl.program_id(0)
+    step = pl.program_id(0)
     count, rows = x_ref.shape[0], x_ref.shape[1]
-    modes = c_ref.shape[1]
+    group, modes, width = c_ref.shape[0], c_ref.shape[1], c_ref.shape[2]
     sgn = sign_row(SUB)
+    low = low_lanes((rows, LANES))
 
     def chunk(c):
         return pl.ds(pl.multiple_of(c * SUB, SUB), SUB)
 
-    @pl.when(tile == 0)
+    @pl.when(step == 0)
     def _():
-        sum_real[...] = jnp.zeros_like(sum_real)
-        sum_imag[...] = jnp.zeros_like(sum_imag)
+        total[...] = jnp.zeros_like(total)
 
         def lanes(q, carry):
             part = pl.ds(q * 4, 4)
@@ -360,33 +366,54 @@
 
         lax.fori_loop(0, rows // SUB, across, 0)
 
-    first, second = spec[2 * tile], spec[2 * tile + 1]
-    low = low_lanes((rows, LANES))
-    real = jnp.where(low, first, swap(second))
-    imag = jnp.where(low, swap(first), second)
-    real_part, imag_part = real[:modes], imag[:modes]
-    for n in range(modes):
-        coup_real, coup_imag = c_ref[0, n], c_ref[1, n]
-        sum_real[n : n + 1, :] = jnp.sum(
-            coup_real * real_part - coup_imag * imag_part, axis=0, keepdims=True
-        )
-        sum_imag[n : n + 1, :] = jnp.sum(
-            coup_real * imag_part + coup_imag * real_part, axis=0, keepdims=True
-        )
-    total_real, total_imag = sum_real[...] + real, sum_imag[...] + imag
-    total_real, total_imag = rotate(
-        total_real, total_imag, spread_cos_ref[...], spread_sin_ref[...]
-    )
-    mixed[2 * tile] = jnp.where(low, total_real, swap(total_imag))
-    mixed[2 * tile + 1] = jnp.where(low, swap(total_real), total_imag)
-
-    @pl.when(tile == pl.num_programs(0) - 1)
+        for tile in range(width // 2):
+            first, second = spec[2 * tile], spec[2 * tile + 1]
+            real = jnp.where(low, first, swap(second))
+            imag = jnp.where(low, swap(first), second)
+            for part in range(2):
+                by_real[pl.ds(2 * tile + part, rows, stride=width), :] = real
+                by_imag[pl.ds(2 * tile + part, rows, stride=width), :] = imag
+
+    odd = lax.broadcasted_iota(jnp.int32, (SUB, LANES), 0) % 2 == 1
+
+    def mix(q, carry):
+        with_real = [jnp.zeros((SUB, LANES), jnp.float32) for _ in range(group)]
+        with_imag = [jnp.zeros((SUB, LANES), jnp.float32) for _ in range(group)]
+        for m in range(modes):
+            at = pl.ds(pl.multiple_of(m * width + q * SUB, SUB), SUB)
+            real, imag = by_real[at, :], by_imag[at, :]
+            for g in range(group):
+                factor = c_ref[g, m, chunk(q), :]
+                with_real[g] = with_real[g] + factor * real
+                with_imag[g] = with_imag[g] + factor * imag
+        for g in range(group):
+            other = jnp.where(
+                odd, pltpu.roll(with_imag[g], 1, 0), -pltpu.roll(with_imag[g], SUB - 1, 0)
+            )
+            at = pl.ds(pl.multiple_of((step * group + g) * width + q * SUB, SUB), SUB)
+            total[at, :] = with_real[g] + other
+        return carry
+
+    lax.fori_loop(0, width // SUB, mix, 0)
+
+    @pl.when(step == pl.num_programs(0) - 1)
     def _():
+        for tile in range(width // 2):
+            first, second = spec[2 * tile], spec[2 * tile + 1]
+            at = pl.ds(tile * LANES, LANES)
+            real = jnp.where(low, first, swap(second)) + total[pl.ds(2 * tile, rows, stride=width), :]
+            imag = jnp.where(low, swap(first), second) + total[
+                pl.ds(2 * tile + 1, rows, stride=width), :
+            ]
+            real, imag = rotate(real, imag, spread_cos_ref[:, at], spread_sin_ref[:, at])
+            spec[2 * tile] = jnp.where(low, real, swap(imag))
+            spec[2 * tile + 1] = jnp.where(low, swap(real), imag)
+
         def across(c, carry):
             rows_of = chunk(c)
-            items = short_fft([mixed[j, rows_of, :] for j in range(count)], 1.0, sgn)
+            items = short_fft([spec[j, rows_of, :] for j in range(count)], 1.0, sgn)
             for p, value in enumerate(items):
-                mixed[p, rows_of, :] = packed_mul(
+                spec[p, rows_of, :] = packed_mul(
                     value, tw_cos_ref[p : p + 1, :], -tw_sin_ref[p : p + 1, :]
                 )
             return carry
@@ -395,7 +422,7 @@
 
         def lanes(q, carry):
             part = pl.ds(q * 4, 4)
-            block = mixed[part].reshape(4 * rows, LANES)
+            block = spec[part].reshape(4 * rows, LANES)
             out_ref[part] = long_dft(block, inv_ref[...]).reshape(4, rows, LANES)
             return carry
 
@@ -404,18 +431,18 @@
 
 def row_stage(x, coupling, spread_cos, spread_sin, tw_cos, tw_sin, fwd, inv):
     rows = x.shape[1]
-    modes = coupling.shape[1]
-    tiles = coupling.shape[3] // LANES
+    modes, width = coupling.shape[0], coupling.shape[2]
+    group = max(g for g in range(1, 7) if modes % g == 0)
     whole = lambda array: pl.BlockSpec(array.shape, lambda t: (0,) * array.ndim)
     return pl.pallas_call(
         row_kernel,
-        grid=(tiles,),
+        grid=(modes // group,),
         out_shape=jax.ShapeDtypeStruct(x.shape, x.dtype),
         in_specs=[
             whole(x),
-            pl.BlockSpec((2, modes, modes, LANES), lambda t: (0, 0, 0, t)),
-            pl.BlockSpec((rows, LANES), lambda t: (0, t)),
-            pl.BlockSpec((rows, LANES), lambda t: (0, t)),
+            pl.BlockSpec((group, modes, width, LANES), lambda t: (t, 0, 0, 0)),
+            whole(spread_cos),
+            whole(spread_sin),
             whole(tw_cos),
             whole(tw_sin),
             whole(fwd),
@@ -424,9 +451,9 @@
         out_specs=whole(x),
         scratch_shapes=[
             pltpu.VMEM(x.shape, jnp.float32),
-            pltpu.VMEM(x.shape, jnp.float32),
-            pltpu.VMEM((rows, LANES), jnp.float32),
-            pltpu.VMEM((rows, LANES), jnp.float32),
+            pltpu.VMEM((rows * width, LANES), jnp.float32),
+            pltpu.VMEM((rows * width, LANES), jnp.float32),
+            pltpu.VMEM((rows * width, LANES), jnp.float32),
         ],
         compiler_params=pltpu.CompilerParams(dimension_semantics=("arbitrary",)),
         name="row",
@@ -481,18 +508,20 @@
     )
     spread_cos, spread_sin = jnp.cos(dispersion), jnp.sin(dispersion)
 
+    coupling = coupling.reshape(2, modes, modes, local // LANES, LANES).transpose(1, 2, 3, 0, 4)
+    coupling = coupling.reshape(modes, modes, 2 * local // LANES, LANES)
     blocks = pulses.reshape(2, modes, groups, shards).transpose(3, 1, 0, 2)
     x = jnp.pad(blocks.reshape(shards, modes, 2 * groups), ((0, 0), (0, pad), (0, 0)))
     scale = 1.0 / total
     for repeat in range(STEPS):
-        x = exchange(x) if repeat == 0 else x
+        x = exchange(x, modes) if repeat == 0 else x
         if repeat == 0:
             x = column_stage(x, twist_cos, twist_sin, gain, scale, False, True)
-        x = exchange(x)
+        x = exchange(x, modes)
         x = row_stage(x, coupling, spread_cos, spread_sin, tw_cos, tw_sin, fwd, inv)
-        x = exchange(x)
+        x = exchange(x, modes)
         x = column_stage(x, twist_cos, twist_sin, gain, scale, True, repeat < STEPS - 1)
-    x = exchange(x)
+    x = exchange(x, modes)
     x = x[:, :modes].reshape(shards, modes, 2, groups).transpose(2, 1, 3, 0)
     return x.reshape(1, 2, modes, local)
 

time: 207 us -> 178 us (0.86)
  local copies, waits for them, and re-layouts: 29.4 us -> 9.27 us
  Pallas kernels: 173 us -> 165 us
    unnamed x1 -> x2, local copies, waits for them, and re-layouts: 19.3 us -> 0.01 us
    pallas_call x8, Pallas kernels: 156 us -> 148 us  [the longest x6 115 us: exchange(): pl.pallas_call(functools.partial(exchange_kernel, count, modes), out_shap...]
where the time goes in v2:
time: 178 us; the launch traced here: 177 us
  Pallas kernels  165 us (93%)
  local copies, waits for them, and re-layouts  9.27 us (5%)
  other arithmetic  2.66 us (1%)
    pallas_call x6, Pallas kernels, exchange(): pl.pallas_call(functools.partial(exchange_kernel, count, modes), out_shap...  115 us
    pallas_call x2, Pallas kernels, row_stage(): pl.pallas_call(row_kernel, grid=(modes // group,), out_shape=jax.ShapeDty...  33.4 us
    pallas_call x3, Pallas kernels, column_stage(): pl.pallas_call(functools.partial(column_kernel, inverse, forward, scale),...  16.5 us

profile of v2, /device:TPU:0, one launch (start us, length us, event | category | flops | bytes accessed | tf_op | source)
XLA Modules:
  0.0 177.0 jit_solution(9133266202925647441)
XLA Ops:
  0.0 0.1 fusion.11
  0.1 0.7 pad_maximum_fusion
  0.8 0.7 pad.13
  1.4 0.7 broadcast_in_dim.2.gain_ref
  2.1 1.9 %reshape.43 = f32[2,30,64,32]{3,2,0,1:T(8,128)S(1)} reshape(f32[1,2,30,2048]{3,1,2,0:T(2,128)} %param.8) | data formatting | bytes 983040 | tf_op jit(solution)/shard_map/reshape | solution.py:513
  4.0 0.7 copy.13
  4.7 0.0 copy-start
  4.7 0.8 pad.12.x_ref
  5.6 21.4 %exchange.6.x_ref = f32[32,32,128]{2,1,0:T(8,128)} custom-call(f32[32,32,128]{2,1,0:T(8,128)} %pad.12.x_ref), custom_call_target="tpu_custom_call" | custom-call | tf_op jit(solution)/shard_map/exchange/pallas_call | solution.py:250
  27.0 3.5 %column.3.x_ref = f32[32,32,128]{2,1,0:T(8,128)} custom-call(f32[32,32,128]{2,1,0:T(8,128)} %exchange.6.x_ref, f32[32,128]{1,0:T(8,128)} %get-tuple-element.15.cos_ref, f32[32,128]{1,0:T(8,128)} %get-tuple-element.16.sin_ref, f32[32,128]{1,0:T(8,128)} %broadcast_in_dim.2.gain_ref), custom_call_target="tpu_custom_call" | custom-call | tf_op jit(solution)/shard_map/column/pallas_call | solution.py:314
  30.4 18.7 %exchange.7.x_ref = f32[32,32,128]{2,1,0:T(8,128)} custom-call(f32[32,32,128]{2,1,0:T(8,128)} %column.3.x_ref), custom_call_target="tpu_custom_call" | custom-call | tf_op jit(solution)/shard_map/exchange/pallas_call | solution.py:250
  49.2 0.0 copy-done
  49.2 1.9 %fusion = (f32[32,2048]{1,0:T(8,128)}, f32[32,2048]{1,0:T(8,128)}) fusion(f32[2048]{0:T(1024)S(1)} %get-tuple-element.14, f32[32]{0:T(128)S(1)} %get-tuple-element.9, f32[2048]{0:T(1024)S(1)} %fusion.13, f32[32]{0:T(128)S(1)} %get-tuple-element.8, f32[2048]{0:T(1024)S(1)} %get-tuple-element.13, f32[32]{0:T(128)S(1)} %get-tuple-element.7), kind=kLoop, calls=%fused_computation.1 | loop fusion | flops 458752 | bytes 549248 | tf_op jit(solution)/shard_map/sin | solution.py:509
  51.1 16.7 %row.2.x_ref = f32[32,32,128]{2,1,0:T(8,128)} custom-call(f32[32,32,128]{2,1,0:T(8,128)} %exchange.7.x_ref, f32[30,30,32,128]{3,2,1,0:T(8,128)} %bitcast.24, f32[32,2048]{1,0:T(8,128)} %get-tuple-element.6.spread_cos_ref, f32[32,2048]{1,0:T(8,128)} %get-tuple-element.5.spread_sin_ref, f32[32,128]{1,0:T(8,128)} %constant.51.clone.tw_cos_ref, ...), custom_call_target="tpu_custom_call" | custom-call | tf_op jit(solution)/shard_map/row/pallas_call | solution.py:437
  67.8 18.7 %exchange.8.x_ref = f32[32,32,128]{2,1,0:T(8,128)} custom-call(f32[32,32,128]{2,1,0:T(8,128)} %row.2.x_ref), custom_call_target="tpu_custom_call" | custom-call | tf_op jit(solution)/shard_map/exchange/pallas_call | solution.py:250
  86.5 7.3 %column.4.x_ref = f32[32,32,128]{2,1,0:T(8,128)} custom-call(f32[32,32,128]{2,1,0:T(8,128)} %exchange.8.x_ref, f32[32,128]{1,0:T(8,128)} %get-tuple-element.15.cos_ref, f32[32,128]{1,0:T(8,128)} %get-tuple-element.16.sin_ref, f32[32,128]{1,0:T(8,128)} %broadcast_in_dim.2.gain_ref), custom_call_target="tpu_custom_call" | custom-call | tf_op jit(solution)/shard_map/column/pallas_call | solution.py:314
  93.8 18.7 %exchange.9.x_ref = f32[32,32,128]{2,1,0:T(8,128)} custom-call(f32[32,32,128]{2,1,0:T(8,128)} %column.4.x_ref), custom_call_target="tpu_custom_call" | custom-call | tf_op jit(solution)/shard_map/exchange/pallas_call | solution.py:250
  112.6 16.7 %row.3.x_ref = f32[32,32,128]{2,1,0:T(8,128)} custom-call(f32[32,32,128]{2,1,0:T(8,128)} %exchange.9.x_ref, f32[30,30,32,128]{3,2,1,0:T(8,128)} %bitcast.25, f32[32,2048]{1,0:T(8,128)} %get-tuple-element.6.spread_cos_ref, f32[32,2048]{1,0:T(8,128)} %get-tuple-element.5.spread_sin_ref, f32[32,128]{1,0:T(8,128)} %constant.51.clone.tw_cos_ref, ...), custom_call_target="tpu_custom_call" | custom-call | tf_op jit(solution)/shard_map/row/pallas_call | solution.py:437
  129.3 18.7 %exchange.10.x_ref = f32[32,32,128]{2,1,0:T(8,128)} custom-call(f32[32,32,128]{2,1,0:T(8,128)} %row.3.x_ref), custom_call_target="tpu_custom_call" | custom-call | tf_op jit(solution)/shard_map/exchange/pallas_call | solution.py:250
  148.0 5.7 %column.5.x_ref = f32[32,32,128]{2,1,0:T(8,128)} custom-call(f32[32,32,128]{2,1,0:T(8,128)} %exchange.10.x_ref, f32[32,128]{1,0:T(8,128)} %get-tuple-element.15.cos_ref, f32[32,128]{1,0:T(8,128)} %get-tuple-element.16.sin_ref, f32[32,128]{1,0:T(8,128)} %broadcast_in_dim.2.gain_ref), custom_call_target="tpu_custom_call" | custom-call | tf_op jit(solution)/shard_map/column/pallas_call | solution.py:314
  153.8 18.7 %exchange.11 = f32[32,32,128]{2,1,0:T(8,128)} custom-call(f32[32,32,128]{2,1,0:T(8,128)} %column.5.x_ref), custom_call_target="tpu_custom_call" | custom-call | tf_op jit(solution)/shard_map/exchange/pallas_call | solution.py:250
  172.5 1.3 copy.15
  173.8 0.6 reshape.47
  174.4 0.8 copy.16
  175.2 1.8 %reshape.48 = f32[1,2,30,2048]{3,1,2,0:T(2,128)} reshape(f32[2,30,64,32]{3,2,0,1:T(8,128)S(1)} %copy.16) | data formatting | bytes 983040 | tf_op jit(solution)/shard_map/reshape | solution.py:526
  (4 shorter events, 0.0 us)
Async XLA Ops:
  4.7 44.5 %copy-start = (f32[3,30]{1,0:T(4,128)S(1)}, f32[3,30]{1,0:T(4,128)}, u32[]{:S(2)}) copy-start(f32[3,30]{1,0:T(4,128)} %param.10) | copy-start | bytes 1084
